TPU v7x, 32 devices: a whole 2x2x4 slice. The times are simulated.
32 devices in a mesh: seq: 4 (over y, x), fsdp: 8 (over z, core).
Axes of the slice: x: 2, y: 2, z: 4, core: 2. Of those that a mesh axis runs over, the one named last changes fastest.
Arguments:
- tokens: bfloat16 [8, 1024, 1536], P('fsdp', 'seq'), may hold values from -6 to 6
- input_projection_weight: bfloat16 [1536, 6448], P('fsdp'), may hold values from -0.15625 to 0.15625
- pre_gain: bfloat16 [1536], P('fsdp'), may hold values from 0.25 to 1.75
- conv_weight: bfloat16 [3328, 4], P('fsdp'), may hold values from -3 to 3
- conv_bias: bfloat16 [3328], P('fsdp'), may hold values from -0.5 to 0.5
- step_bias: bfloat16 [48], P('fsdp'), may hold values from -6 to -1
- decay_log: bfloat16 [48], P('fsdp'), may hold values from 0 to 2.765625
- skip_gain: bfloat16 [48], P('fsdp'), may hold values from 0.5 to 1.5
- post_gain: bfloat16 [3072], P('fsdp'), may hold values from 0.25 to 1.75
- output_projection_weight: bfloat16 [3072, 1536], P(None, 'fsdp'), may hold values from -0.109375 to 0.109375
- cotangent: bfloat16 [8, 1024, 1536], P('fsdp', 'seq'), may hold values from -6 to 6
Outputs:
- block_out: float32 [8, 1024, 1536], P('fsdp', 'seq')
- grad_tokens: float32 [8, 1024, 1536], P('fsdp', 'seq')
- grad_in_weight: float32 [1536, 6448], P('fsdp')
- grad_pre_gain: float32 [1536], P('fsdp')
- grad_conv_weight: float32 [3328, 4], P('fsdp')
- grad_conv_bias: float32 [3328], P('fsdp')
- grad_step_bias: float32 [48], P('fsdp')
- grad_decay_log: float32 [48], P('fsdp')
- grad_skip_gain: float32 [48], P('fsdp')
- grad_post_gain: float32 [3072], P('fsdp')
- grad_out_weight: float32 [3072, 1536], P(None, 'fsdp')
All inputs are finite; a program needn't handle non-finite values.
Results may differ from a plain program's by a relative error of at most 0.012.
The roundings to bfloat16 on the way count: a program that leaves them out, or rounds other values in their place, can miss the bound.
Values may be sent and summed in bfloat16 or wider, within the bound.
A program may use at most 256 MiB of HBM per device.

v0:
```python
import jax
import jax.numpy as jnp
from jax import lax
from jax.sharding import PartitionSpec as P

INNER = 3072
STATE = 128
BLOCK = 256
HEADS = 48


EPS = 1e-05
HIGH_PRECISION = lax.Precision.HIGHEST


def rms_scale(values, gain):
    return values * lax.rsqrt(jnp.mean(values * values, axis=-1, keepdims=True) + EPS) * gain


def conv_silu(signal, kernel, offset):
    tap_count = kernel.shape[1]
    length = signal.shape[1]
    padded = jnp.pad(signal, ((0, 0), (tap_count - 1, 0), (0, 0)))
    summed = offset + jnp.zeros_like(signal)
    for tap_index in range(tap_count):
        summed = summed + padded[:, tap_index : tap_index + length, :] * kernel[:, tap_index]
    return jax.nn.silu(summed)


def block_scan(values, rates, rate_scale, in_map, out_map, block_len):
    seq_count, length, head_count, head_width = values.shape
    block_count = length // block_len
    state_width = in_map.shape[-1]
    val_blocks = values.reshape(seq_count, block_count, block_len, head_count, head_width)
    rate_blocks = rates.reshape(seq_count, block_count, block_len, head_count)
    in_blocks = in_map.reshape(seq_count, block_count, block_len, state_width)
    out_blocks = out_map.reshape(seq_count, block_count, block_len, state_width)
    log_decay = jnp.cumsum(rate_blocks * rate_scale, axis=2)
    affinity = jnp.einsum("bcqn,bcsn->bcqs", out_blocks, in_blocks, precision=HIGH_PRECISION)
    positions = jnp.arange(block_len)
    causal = (positions[:, None] >= positions[None, :])[:, :, None]
    gap_log = log_decay[:, :, :, None, :] - log_decay[:, :, None, :, :]
    within = jnp.where(causal, jnp.exp(jnp.where(causal, gap_log, 0.0)), 0.0)
    mixing = affinity[..., None] * within * rate_blocks[:, :, None, :, :]
    local_out = jnp.einsum("bctsh,bcshp->bcthp", mixing, val_blocks, precision=HIGH_PRECISION)
    last_log = log_decay[:, :, -1, :]
    tail_weight = jnp.exp(last_log[:, :, None, :] - log_decay) * rate_blocks
    states = jnp.einsum(
        "bcsh,bcsn,bcshp->bchpn", tail_weight, in_blocks, val_blocks, precision=HIGH_PRECISION
    )
    through = jnp.cumsum(last_log, axis=1)
    before = through - last_log
    block_ids = jnp.arange(block_count)
    earlier = (block_ids[:, None] > block_ids[None, :])[:, :, None]
    block_gap = before[:, :, None, :] - through[:, None, :, :]
    carry_weight = jnp.where(earlier, jnp.exp(jnp.where(earlier, block_gap, 0.0)), 0.0)
    entering = jnp.einsum("bcdh,bdhpn->bchpn", carry_weight, states, precision=HIGH_PRECISION)
    carried = (
        jnp.einsum("bcqn,bchpn->bcqhp", out_blocks, entering, precision=HIGH_PRECISION)
        * jnp.exp(log_decay)[..., None]
    )
    return (local_out + carried).reshape(seq_count, length, head_count, head_width)


def head_block(
    value_raw,
    state_raw,
    rate_raw,
    kernel_value,
    offset_value,
    kernel_state,
    offset_state,
    step_bias,
    decay_log,
    skip_gain,
):
    values = conv_silu(value_raw, kernel_value, offset_value)
    state_maps = conv_silu(state_raw, kernel_state, offset_state)
    state_width = state_raw.shape[-1] // 2
    rates = jax.nn.softplus(rate_raw + step_bias)
    head_count = rates.shape[-1]
    head_values = values.reshape(values.shape[0], values.shape[1], head_count, -1)
    mixed = block_scan(
        head_values,
        rates,
        -jnp.exp(decay_log),
        state_maps[..., :state_width],
        state_maps[..., state_width:],
        BLOCK,
    )
    mixed = mixed + skip_gain[:, None] * head_values
    return mixed.reshape(values.shape)


def head_sequences(
    value_raw,
    state_raw,
    rate_raw,
    kernel_value,
    offset_value,
    kernel_state,
    offset_state,
    step_bias,
    decay_log,
    skip_gain,
):

    def single_sequence(pieces):
        return head_block(
            pieces[0][None],
            pieces[1][None],
            pieces[2][None],
            kernel_value,
            offset_value,
            kernel_state,
            offset_state,
            step_bias,
            decay_log,
            skip_gain,
        )[0]

    return lax.map(jax.checkpoint(single_sequence), (value_raw, state_raw, rate_raw))


def gate_norm(mixed, gates, gain):
    return rms_scale(mixed * jax.nn.silu(gates), gain)


def own_rows(array, index, row_count):
    return lax.dynamic_slice_in_dim(array, index * row_count, row_count, 0)


def place_rows(full_rows, piece, index):
    zeros_full = jnp.zeros((full_rows,) + piece.shape[1:], jnp.float32)
    return lax.dynamic_update_slice_in_dim(zeros_full, piece, index * piece.shape[0], 0)


def body(
    tokens,
    input_projection_weight,
    pre_gain,
    conv_weight,
    conv_bias,
    step_bias,
    decay_log,
    skip_gain,
    post_gain,
    output_projection_weight,
    cotangent,
):
    head_groups = lax.axis_size("seq")
    head_group = lax.axis_index("seq")
    gathered = (
        lax.all_gather(input_projection_weight, "fsdp", axis=0, tiled=True),
        lax.all_gather(pre_gain, "fsdp", axis=0, tiled=True),
        lax.all_gather(conv_weight, "fsdp", axis=0, tiled=True),
        lax.all_gather(conv_bias, "fsdp", axis=0, tiled=True),
        lax.all_gather(step_bias, "fsdp", axis=0, tiled=True),
        lax.all_gather(decay_log, "fsdp", axis=0, tiled=True),
        lax.all_gather(skip_gain, "fsdp", axis=0, tiled=True),
        lax.all_gather(post_gain, "fsdp", axis=0, tiled=True),
        lax.all_gather(output_projection_weight, "fsdp", axis=1, tiled=True),
    )
    (
        input_weight_whole,
        pre_all,
        kernel_all,
        offset_all,
        bias_all,
        decay_all,
        skip_all,
        post_all,
        output_weight_whole,
    ) = gathered
    residual = tokens.astype(jnp.float32)
    normalized_tokens, pre_pull = jax.vjp(rms_scale, residual, pre_all.astype(jnp.float32))
    normalized_reduced_precision = normalized_tokens.astype(jnp.bfloat16)
    projected_rows = jnp.einsum(
        "ner,ra->nea",
        normalized_reduced_precision,
        input_weight_whole,
        preferred_element_type=jnp.float32,
    ).astype(jnp.bfloat16)
    gate_raw = projected_rows[..., :INNER]
    value_raw = projected_rows[..., INNER : 2 * INNER]
    state_raw = projected_rows[..., 2 * INNER : 2 * INNER + 2 * STATE]
    rate_raw = projected_rows[..., 2 * INNER + 2 * STATE :]
    value_heads, rate_heads = (
        lax.all_to_all(value_raw, "seq", split_axis=2, concat_axis=1, tiled=True),
        lax.all_to_all(rate_raw, "seq", split_axis=2, concat_axis=1, tiled=True),
    )
    state_whole = lax.all_gather(state_raw, "seq", axis=1, tiled=True)
    local_width = INNER // head_groups
    local_heads = HEADS // head_groups
    kernel_value = own_rows(kernel_all, head_group, local_width).astype(jnp.float32)
    offset_value = own_rows(offset_all, head_group, local_width).astype(jnp.float32)
    kernel_state = kernel_all[INNER:].astype(jnp.float32)
    offset_state = offset_all[INNER:].astype(jnp.float32)
    bias_local = own_rows(bias_all, head_group, local_heads).astype(jnp.float32)
    decay_local = own_rows(decay_all, head_group, local_heads).astype(jnp.float32)
    skip_local = own_rows(skip_all, head_group, local_heads).astype(jnp.float32)
    mixed, head_pull = jax.vjp(
        head_sequences,
        value_heads.astype(jnp.float32),
        state_whole.astype(jnp.float32),
        rate_heads.astype(jnp.float32),
        kernel_value,
        offset_value,
        kernel_state,
        offset_state,
        bias_local,
        decay_local,
        skip_local,
    )
    mixed_tokens = lax.all_to_all(
        mixed.astype(jnp.bfloat16), "seq", split_axis=1, concat_axis=2, tiled=True
    )
    reshaped_rows, gate_pull = jax.vjp(
        gate_norm,
        mixed_tokens.astype(jnp.float32),
        gate_raw.astype(jnp.float32),
        post_all.astype(jnp.float32),
    )
    reshaped_reduced_precision = reshaped_rows.astype(jnp.bfloat16)
    block_out = residual + jnp.einsum(
        "vip,pm->vim",
        reshaped_reduced_precision,
        output_weight_whole,
        preferred_element_type=jnp.float32,
    )
    grad_out_full = jnp.einsum(
        "cgh,cgz->hz", reshaped_reduced_precision, cotangent, preferred_element_type=jnp.float32
    )
    gradient_reshaped_rows = jnp.einsum(
        "nox,mx->nom", cotangent, output_weight_whole, preferred_element_type=jnp.float32
    )
    grad_mixed, grad_gate, grad_post_full = gate_pull(gradient_reshaped_rows)
    grad_heads = lax.all_to_all(
        grad_mixed.astype(jnp.bfloat16), "seq", split_axis=2, concat_axis=1, tiled=True
    )
    head_grads = head_pull(grad_heads.astype(jnp.float32))
    grad_value, grad_state, grad_rate = (head_grads[0], head_grads[1], head_grads[2])
    grad_kernel_value, grad_offset_value, grad_kernel_state, grad_offset_state = (
        head_grads[3],
        head_grads[4],
        head_grads[5],
        head_grads[6],
    )
    grad_bias_local, grad_decay_local, grad_skip_local = (
        head_grads[7],
        head_grads[8],
        head_grads[9],
    )
    value_back, rate_back = (
        lax.all_to_all(
            grad_value.astype(jnp.bfloat16), "seq", split_axis=1, concat_axis=2, tiled=True
        ),
        lax.all_to_all(
            grad_rate.astype(jnp.bfloat16), "seq", split_axis=1, concat_axis=2, tiled=True
        ),
    )
    state_back = lax.psum_scatter(grad_state, "seq", scatter_dimension=1, tiled=True).astype(
        jnp.bfloat16
    )
    gradient_projected_rows = jnp.concatenate(
        [grad_gate.astype(jnp.bfloat16), value_back, state_back, rate_back], axis=-1
    )
    grad_in_full = jnp.einsum(
        "mxe,mxo->eo",
        normalized_reduced_precision,
        gradient_projected_rows,
        preferred_element_type=jnp.float32,
    )
    grad_normed = jnp.einsum(
        "atv,uv->atu",
        gradient_projected_rows,
        input_weight_whole,
        preferred_element_type=jnp.float32,
    )
    grad_residual, grad_pre_full = pre_pull(grad_normed)
    grad_tokens = cotangent.astype(jnp.float32) + grad_residual
    grad_kernel_full = jnp.concatenate(
        [place_rows(INNER, grad_kernel_value, head_group), grad_kernel_state], axis=0
    )
    grad_offset_full = jnp.concatenate(
        [place_rows(INNER, grad_offset_value, head_group), grad_offset_state], axis=0
    )
    grad_bias_full = place_rows(HEADS, grad_bias_local, head_group)
    grad_decay_full = place_rows(HEADS, grad_decay_local, head_group)
    grad_skip_full = place_rows(HEADS, grad_skip_local, head_group)
    shards = (
        lax.psum_scatter(grad_in_full, "fsdp", scatter_dimension=0, tiled=True),
        lax.psum_scatter(grad_pre_full, "fsdp", scatter_dimension=0, tiled=True),
        lax.psum_scatter(grad_kernel_full, "fsdp", scatter_dimension=0, tiled=True),
        lax.psum_scatter(grad_offset_full, "fsdp", scatter_dimension=0, tiled=True),
        lax.psum_scatter(grad_bias_full, "fsdp", scatter_dimension=0, tiled=True),
        lax.psum_scatter(grad_decay_full, "fsdp", scatter_dimension=0, tiled=True),
        lax.psum_scatter(grad_skip_full, "fsdp", scatter_dimension=0, tiled=True),
        lax.psum_scatter(grad_post_full, "fsdp", scatter_dimension=0, tiled=True),
        lax.psum_scatter(grad_out_full, "fsdp", scatter_dimension=1, tiled=True),
    )
    shards = lax.psum(
        (
            shards[0],
            shards[1],
            shards[2],
            shards[3],
            shards[4],
            shards[5],
            shards[6],
            shards[7],
            shards[8],
        ),
        "seq",
    )
    (
        grad_in_w,
        grad_pre,
        grad_kernel,
        grad_offset,
        grad_bias,
        grad_decay,
        grad_skip,
        grad_post,
        grad_out_w,
    ) = shards
    return (
        block_out,
        grad_tokens,
        grad_in_w,
        grad_pre,
        grad_kernel,
        grad_offset,
        grad_bias,
        grad_decay,
        grad_skip,
        grad_post,
        grad_out_w,
    )


def solution(mesh):
    in_specs = (
        P("fsdp", "seq", None),
        P("fsdp", None),
        P("fsdp"),
        P("fsdp", None),
        P("fsdp"),
        P("fsdp"),
        P("fsdp"),
        P("fsdp"),
        P("fsdp"),
        P(None, "fsdp"),
        P("fsdp", "seq", None),
    )
    out_specs = (
        P("fsdp", "seq", None),
        P("fsdp", "seq", None),
        P("fsdp", None),
        P("fsdp"),
        P("fsdp", None),
        P("fsdp"),
        P("fsdp"),
        P("fsdp"),
        P("fsdp"),
        P("fsdp"),
        P(None, "fsdp"),
    )
    return jax.shard_map(body, mesh=mesh, in_specs=in_specs, out_specs=out_specs, check_vma=False)
```

profile of v0, /device:TPU:8, one launch (start us, length us, event | category | flops | bytes accessed | tf_op | source)
XLA Modules:
  0.0 1464.5 jit_solution(12479393350467381523)
XLA Ops:
  12.6 28.6 %all-reduce.37 = (bf16[1536]{0:T(1024)(128)(2,1)S(1)}, bf16[48]{0:T(256)(128)(2,1)S(1)}, bf16[48]{0:T(256)(128)(2,1)S(1)}, bf16[3328]{0:T(1024)(128)(2,1)S(1)}, bf16[48]{0:T(256)(128)(2,1)S(1)}) all-reduce(bf16[1536]{0:T(1024)(128)(2,1)S(1)} %dynamic-update-slice.1, ...), channel_id=1, replica_groups=mesh['seq'=4,'fsdp'=8] {'fsdp'}, use_global_device_ids=true, to_apply=%add.24 | all-reduce | flops 5008 | bytes 20032
  41.2 18.5 %all-gather = bf16[8,416,4]{1,2,0:T(4,128)(2,1)S(1)} all-gather(bf16[1,416,4]{1,2,0:T(4,128)(2,1)S(1)} %bitcast.544), channel_id=1, replica_groups=mesh['seq'=4,'fsdp'=8] {'fsdp'}, dimensions={0}, use_global_device_ids=true | all-gather | bytes 29952 | tf_op jit(solution)/shard_map/all_gather | solution.py:156
  62.9 123.7 %all-gather.5.cloned.1.call-done = bf16[1536,6448]{1,0:T(8,128)(2,1)} async-done(((bf16[192,6448]{1,0:T(8,128)(2,1)}), bf16[1536,6448]{1,0:T(8,128)(2,1)}) %all-gather.5.cloned.1.call-update) | async-done | bytes 19808272 | tf_op jit(solution)/shard_map/all_gather | solution.py:154
  186.5 12.6 fusion.16
  205.2 14.1 all_gather.34
  230.9 17.5 %copy.913 = bf16[1,256,3072]{1,0,2:T(2,128)(2,1)S(1)} copy(bf16[1,256,3072]{1,2,0:T(8,128)(2,1)S(1)} %slice.292) | data formatting | bytes 3145728 | tf_op jit(solution)/shard_map/slice | solution.py:185
  248.5 16.7 %reduce.53 = bf16[3072,256]{1,0:T(8,128)(2,1)} reduce(bf16[3072,1,256]{2,1,0:T(2,128)(2,1)S(1)} %bitcast.466, bf16[]{:T(256)} %broadcast.770), dimensions={1}, to_apply=%bitcast.451.reduce_sub_computation | reduce | bytes 3145730
  277.9 13.6 all-to-all-done
  321.1 14.6 fusion.9
  359.1 12.4 reduce.54
  379.8 12.7 all-gather.1
  430.3 18.9 %copy.911 = bf16[1,256,3072]{1,0,2:T(2,128)(2,1)} copy(bf16[1,256,3072]{1,2,0:T(8,128)(2,1)S(1)} %get-tuple-element.428) | data formatting | bytes 3145728 | tf_op jit(solution)/shard_map/convert_element_type | solution.py:239
  449.3 17.8 %reduce.55 = bf16[3072,256]{1,0:T(8,128)(2,1)} reduce(bf16[3072,1,256]{2,1,0:T(2,128)(2,1)} %bitcast.470, bf16[]{:T(256)} %broadcast.770), dimensions={1}, to_apply=%bitcast.449.reduce_sub_computation | reduce | bytes 3145730
  475.2 18.8 %all-to-all-done.3 = bf16[4,2,98304]{2,1,0:T(2,128)(2,1)} async-done(((bf16[4,2,98304]{2,1,0:T(2,128)(2,1)}), bf16[4,2,98304]{2,1,0:T(2,128)(2,1)}, u32[]{:S(2)}, u32[]{:S(2)}) %all-to-all-start.3) | async-done | bytes 1572896 | tf_op jit(solution)/shard_map/all_to_all | solution.py:238
  598.5 23.4 %fusion.18 = (f32[4,256,12]{1,2,0:T(8,128)}, f32[4,256,12]{1,2,0:T(8,128)}, f32[4,256,12]{1,2,0:T(8,128)}, f32[4,256,256]{2,1,0:T(8,128)S(1)}) fusion(f32[4,256,256]{2,1,0:T(8,128)} %copy-done.32, f32[4,256,12]{1,2,0:T(8,128)} %fusion.174, f32[4,256,12]{1,2,0:T(8,128)} %copy.642, pred[256,256]{1,0:T(8,128)(4,1)} %iota_compare_fusion, ...), kind=kOutput, calls=%fused_computation.24 | convolution fusion | flops 2462806016 | bytes 8699904 | tf_op jit(solution)/shard_map/transpose(jvp())/while/body/eval_jaxpr/checkpoint/bctsh,bcshp->bcthp/dot_general | solution.py:45
  668.1 12.0 fusion.215
  732.9 17.7 %all-to-all-done.4 = bf16[4,2,98304]{2,1,0:T(2,128)(2,1)} async-done(((bf16[4,2,98304]{2,1,0:T(2,128)(2,1)}), bf16[4,2,98304]{2,1,0:T(2,128)(2,1)}, u32[]{:S(2)}, u32[]{:S(2)}) %all-to-all-start.4) | async-done | bytes 1572896 | tf_op jit(solution)/shard_map/all_to_all | solution.py:255
  758.1 18.0 %fusion.147 = f32[1536,6448]{1,0:T(8,128)} fusion(bf16[1,256,48]{1,2,0:T(8,128)(2,1)S(1)} %all_to_all.65, bf16[1,256,256]{1,2,0:T(8,128)(2,1)S(1)} %convert_element_type.224, bf16[1,256,3072]{1,2,0:T(8,128)(2,1)S(1)} %bitcast.479, bf16[1,256,3072]{1,2,0:T(8,128)(2,1)} %get-tuple-element.427, bf16[1,256,1536]{2,1,0:T(8,128)(2,1)S(1)} %copy-done.18, ...), kind=kOutput, calls=%fused_computation.188 | convolution fusion | flops 5085691904 | bytes 43711488 | tf_op jit(solution)/shard_map/mxe,mxo->eo/dot_general | solution.py:268
  778.8 87.0 %reduce-scatter.11.cloned.1.call-done = f32[3072,192]{0,1:T(8,128)} async-done(((f32[3072,1536]{0,1:T(8,128)}), f32[3072,192]{0,1:T(8,128)}) %reduce-scatter.11.cloned.1.call-update) | async-done | bytes 2359312 | tf_op jit(solution)/shard_map/reduce_scatter | solution.py:300
  865.8 387.8 %reduce-scatter.9.cloned.1.call-done = f32[192,6448]{1,0:T(8,128)} async-done(((f32[1536,6448]{1,0:T(8,128)}), f32[192,6448]{1,0:T(8,128)}) %reduce-scatter.9.cloned.1.call-update) | async-done | bytes 4952080 | tf_op jit(solution)/shard_map/reduce_scatter | solution.py:292
  1265.7 22.7 %reduce-scatter.13.cloned.1.call-done = f32[416,4]{1,0:T(8,128)} async-done(((f32[3328,4]{1,0:T(8,128)}), f32[416,4]{1,0:T(8,128)}) %reduce-scatter.13.cloned.1.call-update) | async-done | bytes 6672
  1300.7 27.8 %all-reduce.34 = (f32[1536]{0:T(1024)S(1)}, f32[3328]{0:T(1024)S(1)}, f32[48]{0:T(128)S(1)}, f32[48]{0:T(128)S(1)}, f32[48]{0:T(128)S(1)}, /*index=5*/f32[3072]{0:T(1024)S(1)}) all-reduce(f32[1536]{0:T(1024)S(1)} %get-tuple-element.374, f32[3328]{0:T(1024)S(1)} %pad_maximum_fusion.1, ...), channel_id=4, replica_groups=mesh['seq'=4,'fsdp'=8] {'fsdp'}, use_global_device_ids=true, to_apply=%region_25.26.clone | all-reduce | flops 8080 | bytes 64640
  1328.9 17.3 %all-reduce.35 = (f32[192]{0:T(256)}, f32[416,4]{0,1:T(4,128)}, f32[416]{0:T(512)}, f32[6]{0:T(128)}, f32[6]{0:T(128)}, /*index=5*/f32[6]{0:T(128)}, f32[384]{0:T(512)}) all-reduce(f32[192]{0:T(256)S(1)} %dynamic-slice.6, f32[416,4]{0,1:T(4,128)S(1)} %copy.731, f32[416]{0:T(512)S(1)} %dynamic-slice.8, ...), channel_id=1, replica_groups=mesh['seq'=4,'fsdp'=8] {'seq'}, use_global_device_ids=true, to_apply=%region_26.27 | all-reduce | flops 2674 | bytes 21392 | tf_op jit(solution)/shard_map/psum | solution.py:302
  1347.8 103.0 %all-reduce.40.cloned.1.call-done = (f32[192,6448]{1,0:T(8,128)}, f32[3072,192]{0,1:T(8,128)}) async-done(((f32[192,6448]{1,0:T(8,128)}, f32[3072,192]{0,1:T(8,128)}), (f32[192,6448]{1,0:T(8,128)}, f32[3072,192]{0,1:T(8,128)})) %all-reduce.40.cloned.1.call-update) | async-done | bytes 7311376 | tf_op jit(solution)/shard_map/psum | solution.py:302
  (481 shorter events, 386.2 us)
Async XLA Ops:
  7.3 54.2 %copy-start.17 = (bf16[1,256,1536]{2,1,0:T(8,128)(2,1)S(1)}, bf16[1,256,1536]{2,1,0:T(8,128)(2,1)}, u32[]{:S(2)}) copy-start(bf16[1,256,1536]{2,1,0:T(8,128)(2,1)} %param.11) | copy-start | bytes 2359300
  7.3 179.3 %all-gather.5.cloned.1.call-start = ((), (), s32[]{:S(2)}) async-start(), calls=%async_computation.10 | async-start | bytes 22560768 | tf_op jit(solution)/shard_map/all_gather | solution.py:154
  8.0 407.8 %all-gather.7.cloned.1.call-start = ((), (), s32[]{:S(2)}) async-start(), calls=%async_computation.11 | async-start | bytes 10616832 | tf_op jit(solution)/shard_map/all_gather | solution.py:162
  41.2 158.0 %copy-start.36 = (f32[1536]{0:T(1024)}, f32[1536]{0:T(1024)S(1)}, u32[]{:S(2)}) copy-start(f32[1536]{0:T(1024)S(1)} %convert_element_type.185) | copy-start | bytes 18436
  59.9 446.2 %copy-start.56 = (f32[12]{0:T(128)}, f32[12]{0:T(128)S(1)}, u32[]{:S(2)}) copy-start(f32[12]{0:T(128)S(1)} %get-tuple-element.355) | copy-start | bytes 148
  60.0 257.4 %copy-start.68 = (pred[4,4]{1,0:T(4,128)(4,1)}, pred[4,4]{1,0:T(4,128)(4,1)S(1)}, u32[]{:S(2)}) copy-start(pred[4,4]{1,0:T(4,128)(4,1)S(1)} %iota_compare_fusion.1) | copy-start | bytes 52
  60.8 290.6 %copy-start.48 = (f32[768]{0:T(1024)}, f32[768]{0:T(1024)S(1)}, u32[]{:S(2)}) copy-start(f32[768]{0:T(1024)S(1)} %dynamic-slice_convert_fusion.1) | copy-start | bytes 9220
  62.3 136.9 %copy-start.57 = (f32[256]{0:T(256)}, f32[256]{0:T(256)S(1)}, u32[]{:S(2)}) copy-start(f32[256]{0:T(256)S(1)} %fusion.204) | copy-start | bytes 3076
  62.9 136.3 %copy-start.54 = (f32[256,4]{0,1:T(4,128)}, f32[256,4]{0,1:T(4,128)S(1)}, u32[]{:S(2)}) copy-start(f32[256,4]{0,1:T(4,128)S(1)} %slice_convert_fusion) | copy-start | bytes 12292
  201.3 67.6 %all-to-all-start.1 = ((bf16[4,2,1536]{2,1,0:T(2,128)(2,1)}), bf16[4,2,1536]{2,1,0:T(2,128)(2,1)S(1)}, u32[]{:S(2)}, u32[]{:S(2)}) async-start(bf16[4,2,1536]{2,1,0:T(2,128)(2,1)} %reshape.1399), calls=%async_computation.1 | async-start | bytes 49152 | tf_op jit(solution)/shard_map/all_to_all | solution.py:190
  268.9 22.6 %all-to-all-start = ((bf16[4,2,98304]{2,1,0:T(2,128)(2,1)}), bf16[4,2,98304]{2,1,0:T(2,128)(2,1)}, u32[]{:S(2)}, u32[]{:S(2)}) async-start(bf16[4,2,98304]{2,1,0:T(2,128)(2,1)} %reshape.1401), calls=%async_computation | async-start | bytes 3145728 | tf_op jit(solution)/shard_map/all_to_all | solution.py:189
  375.2 23.3 %all-to-all-start.2 = ((bf16[4,2,98304]{2,1,0:T(2,128)(2,1)}), bf16[4,2,98304]{2,1,0:T(2,128)(2,1)}, u32[]{:S(2)}, u32[]{:S(2)}) async-start(bf16[4,2,98304]{2,1,0:T(2,128)(2,1)} %reshape.1403), calls=%async_computation.2 | async-start | bytes 3145728 | tf_op jit(solution)/shard_map/all_to_all | solution.py:215
  470.8 23.2 %all-to-all-start.3 = ((bf16[4,2,98304]{2,1,0:T(2,128)(2,1)}), bf16[4,2,98304]{2,1,0:T(2,128)(2,1)}, u32[]{:S(2)}, u32[]{:S(2)}) async-start(bf16[4,2,98304]{2,1,0:T(2,128)(2,1)} %reshape.1405), calls=%async_computation.3 | async-start | bytes 3145728 | tf_op jit(solution)/shard_map/all_to_all | solution.py:238
  475.1 281.8 %reduce-scatter.7.cloned.1.call-start = ((), (), s32[]{:S(2)}) async-start(), calls=%async_computation.12 | async-start | bytes 1310720 | tf_op jit(solution)/shard_map/reduce_scatter | solution.py:262
  544.2 123.4 %copy-start.40 = (f32[4,12]{1,0:T(4,128)}, f32[4,12]{1,0:T(4,128)S(1)}, u32[]{:S(2)}) copy-start(f32[4,12]{1,0:T(4,128)S(1)} %slice_reduce_fusion) | copy-start | bytes 580
  650.4 215.4 %reduce-scatter.11.cloned.1.call-start = ((), (), s32[]{:S(2)}) async-start(), calls=%async_computation.14 | async-start | bytes 21233664 | tf_op jit(solution)/shard_map/reduce_scatter | solution.py:300
  703.3 24.1 %all-to-all-start.5 = ((bf16[4,2,1536]{2,1,0:T(2,128)(2,1)}), bf16[4,2,1536]{2,1,0:T(2,128)(2,1)S(1)}, u32[]{:S(2)}, u32[]{:S(2)}) async-start(bf16[4,2,1536]{2,1,0:T(2,128)(2,1)} %reshape.1407), calls=%async_computation.6 | async-start | bytes 49152 | tf_op jit(solution)/shard_map/all_to_all | solution.py:258
  727.4 23.2 %all-to-all-start.4 = ((bf16[4,2,98304]{2,1,0:T(2,128)(2,1)}), bf16[4,2,98304]{2,1,0:T(2,128)(2,1)}, u32[]{:S(2)}, u32[]{:S(2)}) async-start(bf16[4,2,98304]{2,1,0:T(2,128)(2,1)} %reshape.1409), calls=%async_computation.4 | async-start | bytes 3145728 | tf_op jit(solution)/shard_map/all_to_all | solution.py:255
  731.8 521.8 %reduce-scatter.9.cloned.1.call-start = ((), (), s32[]{:S(2)}) async-start(), calls=%async_computation.13 | async-start | bytes 45121536 | tf_op jit(solution)/shard_map/reduce_scatter | solution.py:292
  776.2 512.2 %reduce-scatter.13.cloned.1.call-start = ((), (), s32[]{:S(2)}) async-start(), calls=%async_computation.15 | async-start | bytes 1916928
  778.8 672.1 %all-reduce.40.cloned.1.call-start = ((), (), s32[]{:S(2)}) async-start(), calls=%async_computation.16 | async-start | bytes 14745600 | tf_op jit(solution)/shard_map/psum | solution.py:302
  1289.5 56.7 %copy-start.72 = (f32[256]{0:T(256)S(1)}, f32[256]{0:T(256)}, u32[]{:S(2)}) copy-start(f32[256]{0:T(256)} %copy-done.71) | copy-start | bytes 3076
  1289.5 56.7 %copy-start.19 = (bf16[1,256,1536]{2,1,0:T(8,128)(2,1)S(1)}, bf16[1,256,1536]{2,1,0:T(8,128)(2,1)}, u32[]{:S(2)}) copy-start(bf16[1,256,1536]{2,1,0:T(8,128)(2,1)} %param.11) | copy-start | bytes 2359300
  1289.5 56.7 %copy-start.28 = (bf16[1,256,1536]{2,1,0:T(8,128)(2,1)S(1)}, bf16[1,256,1536]{2,1,0:T(8,128)(2,1)}, u32[]{:S(2)}) copy-start(bf16[1,256,1536]{2,1,0:T(8,128)(2,1)} %param.21) | copy-start | bytes 2359300
  (90 other events, 589.5 us)
Sparse Core Ops, SparseCore 0:
  9.7 176.7 all-gather.4
  188.2 89.0 all-gather.6
  650.5 27.9 reduce-scatter.6
  680.7 185.0 reduce-scatter.10
  868.0 385.4 reduce-scatter.8
  1256.3 32.1 reduce-scatter.12
  1292.0 158.8 all-reduce.39
where the time goes:
time: 1470 us; the launch traced here: 1460 us
  waiting for transfers between devices  782 us (53%)
  local copies, waits for them, and re-layouts  188 us (13%)
  matrix products  182 us (12%)
  other arithmetic  147 us (10%)
  blocking collectives  119 us (8%)
  starting transfers between devices  25.6 us (2%)
  between operations  21.1 us (1%)
    reduce_scatter x1, waiting for transfers between devices, body(): lax.psum_scatter(grad_in_full, 'fsdp', scatter_dimension=0, tiled=True)  388 us
    all_gather x1, waiting for transfers between devices, body(): lax.all_gather(input_projection_weight, 'fsdp', axis=0, tiled=True)  124 us
    psum x1, waiting for transfers between devices, body(): lax.psum((shards[0], shards[1], shards[2], shards[3], shards[4], shards[5...  103 us
    reduce_scatter x1, waiting for transfers between devices, body(): lax.psum_scatter(grad_out_full, 'fsdp', scatter_dimension=1, tiled=True)  87 us
    unnamed x7, other arithmetic  67.9 us
    unnamed x2, blocking collectives  56.4 us
    unnamed x246, local copies, waits for them, and re-layouts  50.8 us
    dot_general x3, matrix products, block_scan(): jnp.einsum('bctsh,bcshp->bcthp', mixing, val_blocks, precision=HIGH_PRECI...  50 us
  transfers between devices with their start and end apart: 13, of which 9 were waited for; matrix products, arithmetic and copies ran while one was open for 20% of the time, Pallas kernels for 0%

commit v1 on v0

v1 whole, which is shorter than its diff:
```python
import functools

import jax
import jax.numpy as jnp
from jax import lax
from jax.experimental import pallas as pl
from jax.experimental.pallas import tpu as pltpu
from jax.sharding import PartitionSpec as P

D = 1536
INNER = 3072
STATE = 128
HEADS = 48
XBC = INNER + 2 * STATE
EPS = 1e-05

SEQ = 4
W = INNER // SEQ
HL = HEADS // SEQ
HW = INNER // HEADS
CH = W + 2 * STATE
VC = CH + 128
Q = 128

F32 = jnp.float32
BF16 = jnp.bfloat16
MESH = pl.DeviceIdType.MESH
HIGH = lax.Precision.HIGHEST
VMEM = pl.BlockSpec(memory_space=pltpu.VMEM)
ANY = pl.BlockSpec(memory_space=pl.ANY)
VMEM_LIMIT = 64000 * 1024


def rcopy(src, dst, send_sem, recv_sem, device):
    return pltpu.make_async_remote_copy(
        src_ref=src, dst_ref=dst, send_sem=send_sem, recv_sem=recv_sem, device_id=device, device_id_type=MESH
    )


def signal(sem, device):
    pl.semaphore_signal(sem, inc=1, device_id=device, device_id_type=MESH)


def nn(a, b, precision=None):
    return lax.dot_general(a, b, (((1,), (0,)), ((), ())), precision=precision, preferred_element_type=F32)


def nt(a, b, precision=None):
    return lax.dot_general(a, b, (((1,), (1,)), ((), ())), precision=precision, preferred_element_type=F32)


def seq_gather_start(refs, outs, send, recv, px, py, me):
    for g, (src, out) in enumerate(zip(refs, outs)):
        n = src.shape[0]
        own = out.at[pl.ds(me * n, n)]
        rcopy(src, own, send.at[g, 0], recv.at[g, 0], {"seq": px}).start()
        rcopy(src, own, send.at[g, 1], recv.at[g, 1], {"seq": py}).start()


def seq_gather_relay(g, src, out, send, recv, px, py, me):
    n = src.shape[0]
    h = n // 2
    own = out.at[pl.ds(me * n, n)]
    rcopy(src, own, send.at[g, 0], recv.at[g, 0], {"seq": px}).wait_recv()
    top = out.at[pl.ds(px * n, h)]
    rcopy(top, top, send.at[g, 2], recv.at[g, 2], {"seq": py}).start()
    rcopy(src, own, send.at[g, 1], recv.at[g, 1], {"seq": py}).wait_recv()
    low = out.at[pl.ds(py * n + h, h)]
    rcopy(low, low, send.at[g, 3], recv.at[g, 3], {"seq": px}).start()


def seq_gather_finish(g, src, out, send, recv, px, py, me):
    n = src.shape[0]
    h = n // 2
    own = out.at[pl.ds(me * n, n)]
    half = out.at[pl.ds(me * n, h)]
    rcopy(half, half, send.at[g, 2], recv.at[g, 2], {"seq": py}).wait()
    rcopy(half, half, send.at[g, 3], recv.at[g, 3], {"seq": px}).wait()
    rcopy(src, own, send.at[g, 0], recv.at[g, 0], {"seq": px}).wait_send()
    rcopy(src, own, send.at[g, 1], recv.at[g, 1], {"seq": py}).wait_send()


def gather_kernel(nf, tok, cot, w0, w1, w2, small, tok_all, cot_all, g0, g1, g2, small_all, xs, xr, zs, zr, ms, mr, ls):
    s = lax.axis_index("seq")
    f = lax.axis_index("fsdp")
    px, py = s ^ 1, s ^ 2
    nl = nf // 2
    p, c = f // 2, f % 2
    partner = p * 2 + 1 - c
    bar = pltpu.get_barrier_semaphore()
    signal(bar, {"seq": px})
    signal(bar, {"seq": py})
    for k in range(1, nf):
        signal(bar, {"fsdp": lax.rem(f + k, nf)})
    pl.semaphore_wait(bar, nf + 1)

    ns = small.shape[0]
    own_small = small_all.at[pl.ds(f * ns, ns)]
    for k in range(1, nf):
        rcopy(small, own_small, ms.at[k], mr.at[k], {"fsdp": lax.rem(f + k, nf)}).start()
    seq_gather_start((tok, cot), (tok_all, cot_all), xs, xr, px, py, s)

    ins, outs = (w0, w1, w2), (g0, g1, g2)
    n = w0.shape[0]

    def row(g, i):
        return outs[g].at[pl.ds(i * n, n)]

    def hop(g, src, i, way, k, device):
        return rcopy(src, row(g, i), zs.at[g, way, k], zr.at[g, i], {"fsdp": device})

    locals_ = [
        pltpu.make_async_copy(small, own_small, ls.at[0]),
        pltpu.make_async_copy(tok, tok_all.at[pl.ds(s * tok.shape[0], tok.shape[0])], ls.at[1]),
        pltpu.make_async_copy(cot, cot_all.at[pl.ds(s * cot.shape[0], cot.shape[0])], ls.at[2]),
    ]
    for g in range(3):
        @pl.when(p < nl - 1)
        def _():
            hop(g, ins[g], f, 0, 0, f + 2).start()

        @pl.when(p > 0)
        def _():
            hop(g, ins[g], f, 1, 0, f - 2).start()

        hop(g, ins[g], f, 2, 0, partner).start()
        locals_.append(pltpu.make_async_copy(ins[g], row(g, f), ls.at[3 + g]))
    for copy in locals_:
        copy.start()
    seq_gather_relay(0, tok, tok_all, xs, xr, px, py, s)

    for g in range(3):
        for k in range(1, nl):
            @pl.when(p - k >= 0)
            def _():
                o = f - 2 * k
                hop(g, row(g, o), o, 0, k, f).wait_recv()

                @pl.when(p < nl - 1)
                def _():
                    hop(g, row(g, o), o, 0, k, f + 2).start()

                hop(g, row(g, o), o, 2, k, partner).start()

            @pl.when(p + k < nl)
            def _():
                o = f + 2 * k
                hop(g, row(g, o), o, 1, k, f).wait_recv()

                @pl.when(p > 0)
                def _():
                    hop(g, row(g, o), o, 1, k, f - 2).start()

                hop(g, row(g, o), o, 3, k, partner).start()

        if g == 1:
            seq_gather_relay(1, cot, cot_all, xs, xr, px, py, s)

    for copy in locals_:
        copy.wait()
    for k in range(1, nf):
        rcopy(small, own_small, ms.at[k], mr.at[k], {"fsdp": lax.rem(f + k, nf)}).wait()
    seq_gather_finish(0, tok, tok_all, xs, xr, px, py, s)
    seq_gather_finish(1, cot, cot_all, xs, xr, px, py, s)
    for g in range(3):
        for q in range(nl):
            o = q * 2 + 1 - c
            hop(g, row(g, o), o, 2, 0, partner).wait_recv()
        hop(g, ins[g], f, 2, 0, partner).wait_send()

        @pl.when(p < nl - 1)
        def _():
            hop(g, ins[g], f, 0, 0, f + 2).wait_send()

        @pl.when(p > 0)
        def _():
            hop(g, ins[g], f, 1, 0, f - 2).wait_send()

        for k in range(1, nl):
            @pl.when(p - k >= 0)
            def _():
                o = f - 2 * k

                @pl.when(p < nl - 1)
                def _():
                    hop(g, row(g, o), o, 0, k, f + 2).wait_send()

                hop(g, row(g, o), o, 2, k, partner).wait_send()

            @pl.when(p + k < nl)
            def _():
                o = f + 2 * k

                @pl.when(p > 0)
                def _():
                    hop(g, row(g, o), o, 1, k, f - 2).wait_send()

                hop(g, row(g, o), o, 3, k, partner).wait_send()


def gather_all(nf, tok, cot, w0, w1, w2, small):
    shape = jax.ShapeDtypeStruct
    dma = pltpu.SemaphoreType.DMA
    return pl.pallas_call(
        functools.partial(gather_kernel, nf),
        out_shape=[
            shape((SEQ * tok.shape[0], D), BF16),
            shape((SEQ * tok.shape[0], D), BF16),
            shape((nf * w0.shape[0], w0.shape[1]), BF16),
            shape((nf * w1.shape[0], w1.shape[1]), BF16),
            shape((nf * w2.shape[0], w2.shape[1]), BF16),
            shape((nf * small.shape[0], 128), F32),
        ],
        in_specs=[ANY] * 6,
        out_specs=[ANY] * 6,
        scratch_shapes=[
            dma((2, 4)),
            dma((2, 4)),
            dma((3, 4, nf // 2)),
            dma((3, nf)),
            dma((nf,)),
            dma((nf,)),
            dma((6,)),
        ],
        name="gather_all",
        compiler_params=pltpu.CompilerParams(collective_id=1, has_side_effects=True),
    )(tok, cot, w0, w1, w2, small)


def stats_kernel(a, out, got, send, recv):
    s = lax.axis_index("seq")
    bar = pltpu.get_barrier_semaphore()
    for k in range(1, SEQ):
        signal(bar, {"seq": s ^ k})
    pl.semaphore_wait(bar, SEQ - 1)
    copies = [rcopy(a, got.at[k], send.at[k], recv.at[k], {"seq": s ^ k}) for k in range(1, SEQ)]
    for copy in copies:
        copy.start()
    for copy in copies:
        copy.wait()
    out[...] = a[...] + got[1] + (got[2] + got[3])


def stats_sum(a):
    dma = pltpu.SemaphoreType.DMA
    return pl.pallas_call(
        stats_kernel,
        out_shape=jax.ShapeDtypeStruct(a.shape, F32),
        in_specs=[VMEM],
        out_specs=VMEM,
        scratch_shapes=[pltpu.VMEM((SEQ,) + a.shape, F32), dma((SEQ,)), dma((SEQ,))],
        name="stats_sum",
        compiler_params=pltpu.CompilerParams(collective_id=2, has_side_effects=True),
    )(a)


def softplus(x):
    return jnp.maximum(x, 0.0) + jnp.log1p(jnp.exp(-jnp.abs(x)))


def sigmoid(x):
    return 1.0 / (1.0 + jnp.exp(-x))


def rates_of(r_ref, rows, hp_ref, tri):
    raw = r_ref[rows, :].astype(F32) + hp_ref[0:1, :]
    dt = softplus(raw)
    lam = nn(tri, dt * hp_ref[1:2, :], HIGH)
    return raw, dt, lam


def spread(mat, h):
    return jnp.broadcast_to(mat[:, h : h + 1], (mat.shape[0], 128))


def scan_fwd_kernel(v_ref, s_ref, r_ref, kw_ref, hp_ref, ex_ref, mixed_ref, k_ref, st_ref, buf, hst, xw_s, er_s):
    blocks = v_ref.shape[0] // Q
    row = lax.broadcasted_iota(jnp.int32, (Q, Q), 0)
    col = lax.broadcasted_iota(jnp.int32, (Q, Q), 1)
    causal = row >= col
    tri = causal.astype(F32)
    low = lax.broadcasted_iota(jnp.int32, (Q, 128), 1) < HW
    low1 = lax.broadcasted_iota(jnp.int32, (1, 128), 1) < HW
    buf[0:8, :] = jnp.zeros((8, CH), F32)
    hst[...] = jnp.zeros_like(hst)

    def block(b, carry):
        rows = pl.ds(pl.multiple_of(b * Q, Q), Q)
        buf[8 : 8 + Q, 0:W] = v_ref[rows, :].astype(F32)
        buf[8 : 8 + Q, W:CH] = s_ref[rows, :].astype(F32)
        k = kw_ref[4:5, :] + buf[5 : 5 + Q, :] * kw_ref[0:1, :]
        for j in range(1, 4):
            k = k + buf[5 + j : 5 + j + Q, :] * kw_ref[j : j + 1, :]
        k_ref[rows, :] = k
        buf[0:8, :] = buf[Q : Q + 8, :]
        x = k * sigmoid(k)
        bs, cs = x[:, W : W + STATE], x[:, W + STATE :]
        _, dt, lam = rates_of(r_ref, rows, hp_ref, tri)
        lam_t, dt_t = lam.T, dt.T
        last = lam[Q - 1 : Q, :]
        tail = dt * jnp.exp(last - lam)
        aff = nt(cs, bs, HIGH)
        st_ref[b] = hst[...].astype(BF16)
        ch = nn(cs.astype(BF16), st_ref[b])
        for i in range(HL // 2):
            at = slice(128 * i, 128 * i + 128)
            xp = x[:, at]
            xb = xp.astype(BF16)
            y, lc = [], []
            for h in (2 * i, 2 * i + 1):
                lcol = spread(lam, h)
                within = jnp.exp(jnp.where(causal, lcol - lam_t[h : h + 1, :], -1e30))
                y.append(nn((aff * within * dt_t[h : h + 1, :]).astype(BF16), xb))
                lc.append(lcol)
            out = jnp.where(low, y[0], y[1])
            out = out + jnp.exp(jnp.where(low, lc[0], lc[1])) * ch[:, at] + ex_ref[0:1, at] * xp
            mixed_ref[rows, at] = out.astype(BF16)
            xw_s[:, at] = (xp * jnp.where(low, spread(tail, 2 * i), spread(tail, 2 * i + 1))).astype(BF16)
            er_s[0:1, at] = jnp.exp(jnp.where(low1, spread(last, 2 * i), spread(last, 2 * i + 1)))
        hst[...] = hst[...] * er_s[0:1, :] + nn(bs.T.astype(BF16), xw_s[...])
        return carry

    lax.fori_loop(0, blocks, block, 0)


def scan_fwd(v, s, r, kw, hp, ex):
    length = v.shape[0]
    shape = jax.ShapeDtypeStruct
    return pl.pallas_call(
        scan_fwd_kernel,
        out_shape=[shape((length, W), BF16), shape((length, CH), F32), shape((length // Q, STATE, W), BF16)],
        in_specs=[VMEM] * 6,
        out_specs=[VMEM] * 3,
        scratch_shapes=[
            pltpu.VMEM((Q + 8, CH), F32),
            pltpu.VMEM((STATE, W), F32),
            pltpu.VMEM((Q, W), BF16),
            pltpu.VMEM((8, W), F32),
        ],
        name="scan_fwd",
        compiler_params=pltpu.CompilerParams(vmem_limit_bytes=VMEM_LIMIT),
    )(v, s, r, kw, hp, ex)


def scan_bwd_kernel(
    v_ref, s_ref, r_ref, k_ref, dy_ref, st_ref, kw_ref, hp_ref, ex_ref,
    dv_ref, gcw_ref, gch_ref, ghd_ref,
    buf, dhst, rowp, xw_s, e_s, er_s,
):
    blocks = v_ref.shape[0] // Q
    row = lax.broadcasted_iota(jnp.int32, (Q, Q), 0)
    col = lax.broadcasted_iota(jnp.int32, (Q, Q), 1)
    tri = (row >= col).astype(F32)
    later = col >= row
    suffix = later.astype(F32)
    strict = (col < row).astype(F32)
    lane = lax.broadcasted_iota(jnp.int32, (Q, 128), 1)
    lane1 = lax.broadcasted_iota(jnp.int32, (1, 128), 1)
    low = lane < HW
    low1 = lane1 < HW
    buf[Q : Q + 8, :] = jnp.zeros((8, CH), F32)
    dhst[...] = jnp.zeros_like(dhst)
    rowp[...] = jnp.zeros_like(rowp)
    gcw_ref[...] = jnp.zeros_like(gcw_ref)
    gch_ref[...] = jnp.zeros_like(gch_ref)
    ghd_ref[...] = jnp.zeros_like(ghd_ref)

    def block(i0, carry):
        b = blocks - 1 - i0
        rows = pl.ds(pl.multiple_of(b * Q, Q), Q)
        k = k_ref[rows, :]
        sg = sigmoid(k)
        x = k * sg
        ds = sg * (1.0 + k * (1.0 - sg))
        bs, cs = x[:, W : W + STATE], x[:, W + STATE :]
        bb, cb = bs.astype(BF16), cs.astype(BF16)
        raw, dt, lam = rates_of(r_ref, rows, hp_ref, tri)
        lam_t = lam.T
        last = lam[Q - 1 : Q, :]
        aff_t = nt(bs, cs, HIGH)
        hb = st_ref[b]
        dhb = dhst[...].astype(BF16)
        ch = nn(cb, hb)
        bd = nn(bb, dhb)
        daff_t = jnp.zeros((Q, Q), F32)
        col_n = jnp.zeros((Q, 128), F32)
        col_i = jnp.zeros((Q, 128), F32)
        row_i = jnp.zeros((Q, 128), F32)
        through = jnp.zeros((1, 128), F32)
        for i in range(HL // 2):
            at = slice(128 * i, 128 * i + 128)
            xp = x[:, at]
            xb = xp.astype(BF16)
            dyb = dy_ref[rows, at]
            dyf = dyb.astype(F32)
            z, lc, dc = [], [], []
            for h in (2 * i, 2 * i + 1):
                mine = low if h % 2 == 0 else jnp.logical_not(low)
                lcol, dcol = spread(lam, h), spread(dt, h)
                within = jnp.exp(jnp.where(later, lam_t[h : h + 1, :] - lcol, -1e30))
                g = nt(jnp.where(mine, xp, 0.0).astype(BF16), dyb)
                lg = within * g
                lgd = lg * dcol
                daff_t = daff_t + lgd
                col_n = jnp.where(lane == h, jnp.sum(aff_t * lg, axis=1, keepdims=True), col_n)
                rowp[h : h + 1, :] = jnp.sum(aff_t * lgd, axis=0, keepdims=True)
                z.append(nn((aff_t * within).astype(BF16), dyb))
                lc.append(lcol)
                dc.append(dcol)
            lamp = jnp.where(low, lc[0], lc[1])
            dtp = jnp.where(low, dc[0], dc[1])
            lastp = jnp.where(low1, spread(last, 2 * i), spread(last, 2 * i + 1))
            e = dyf * jnp.exp(lamp)
            e_s[:, at] = e.astype(BF16)
            ew = jnp.exp(lastp - lamp)
            bdp = bd[:, at]
            xw_s[:, at] = (xp * (dtp * ew)).astype(BF16)
            er_s[0:1, at] = jnp.exp(lastp)
            re = e * ch[:, at]
            ci = xp * bdp * ew
            th = jnp.sum(dhst[:, at] * hb[:, at].astype(F32), axis=0, keepdims=True) * er_s[0:1, at]
            for h in (2 * i, 2 * i + 1):
                mine = low if h % 2 == 0 else jnp.logical_not(low)
                mine1 = low1 if h % 2 == 0 else jnp.logical_not(low1)
                row_i = jnp.where(lane == h, jnp.sum(jnp.where(mine, re, 0.0), axis=1, keepdims=True), row_i)
                col_i = jnp.where(lane == h, jnp.sum(jnp.where(mine, ci, 0.0), axis=1, keepdims=True), col_i)
                through = jnp.where(
                    lane1 == h, jnp.sum(jnp.where(mine1, th, 0.0), axis=1, keepdims=True), through
                )
            dx = dtp * jnp.where(low, z[0], z[1]) + bdp * (dtp * ew) + ex_ref[0:1, at] * dyf
            gch_ref[0:1, at] += jnp.sum(dyf * xp, axis=0, keepdims=True)
            buf[0:Q, at] = dx * ds[:, at]
        daff_b = daff_t.astype(BF16)
        d_bs = nt(xw_s[...], dhb) + nn(daff_b, cb)
        d_cs = nt(e_s[...], hb) + nn(daff_t.T.astype(BF16), bb)
        buf[0:Q, W : W + STATE] = d_bs * ds[:, W : W + STATE]
        buf[0:Q, W + STATE : CH] = d_cs * ds[:, W + STATE :]
        dhst[...] = dhst[...] * er_s[0:1, :] + nn(cs.T.astype(BF16), e_s[...])
        after = nn(suffix, rowp[...].T - dt * col_n + row_i, HIGH) + nn(strict, dt * col_i, HIGH) + through
        d_rate = (col_n + col_i + hp_ref[1:2, :] * after) * sigmoid(raw)
        ghd_ref[0:1, :] += jnp.sum(d_rate, axis=0, keepdims=True)
        ghd_ref[1:2, :] += jnp.sum(dt * after, axis=0, keepdims=True) * hp_ref[1:2, :]
        dv_ref[rows, CH:VC] = d_rate.astype(BF16)
        for at, ref in ((slice(0, W), v_ref), (slice(W, CH), s_ref)):
            raw_v = ref[rows, :].astype(F32)
            dk = buf[0:Q, at]
            dv = dk * kw_ref[3:4, at]
            gcw_ref[4:5, at] += jnp.sum(dk, axis=0, keepdims=True)
            gcw_ref[3:4, at] += jnp.sum(dk * raw_v, axis=0, keepdims=True)
            for j in range(3):
                dk = buf[3 - j : 3 - j + Q, at]
                dv = dv + dk * kw_ref[j : j + 1, at]
                gcw_ref[j : j + 1, at] += jnp.sum(dk * raw_v, axis=0, keepdims=True)
            dv_ref[rows, at] = dv.astype(BF16)
        buf[Q : Q + 8, :] = buf[0:8, :]
        return carry

    lax.fori_loop(0, blocks, block, 0)


def scan_bwd(v, s, r, k, dy, st, kw, hp, ex):
    length = v.shape[0]
    shape = jax.ShapeDtypeStruct
    return pl.pallas_call(
        scan_bwd_kernel,
        out_shape=[shape((length, VC), BF16), shape((8, CH), F32), shape((8, W), F32), shape((8, 128), F32)],
        in_specs=[VMEM] * 9,
        out_specs=[VMEM] * 4,
        scratch_shapes=[
            pltpu.VMEM((Q + 8, CH), F32),
            pltpu.VMEM((STATE, W), F32),
            pltpu.VMEM((128, Q), F32),
            pltpu.VMEM((Q, W), BF16),
            pltpu.VMEM((Q, W), BF16),
            pltpu.VMEM((8, W), F32),
        ],
        name="scan_bwd",
        compiler_params=pltpu.CompilerParams(vmem_limit_bytes=VMEM_LIMIT),
    )(v, s, r, k, dy, st, kw, hp, ex)


def reduce_kernel(nf, *refs):
    ins, outs = refs[:6], refs[6:12]
    pb, ub, db, cs, own = refs[12:16], refs[16:20], refs[20:24], refs[24:28], refs[28:32]
    ab, az = refs[32:34], refs[34:36]
    zs, zr, xs, xr, as_, ar, ls = refs[36:]
    s = lax.axis_index("seq")
    f = lax.axis_index("fsdp")
    px, py = s ^ 1, s ^ 2
    nl = nf // 2
    p, c = f // 2, f % 2
    partner = p * 2 + 1 - c
    bar = pltpu.get_barrier_semaphore()
    signal(bar, {"seq": px})
    signal(bar, {"seq": py})
    signal(bar, {"fsdp": partner})

    @pl.when(p < nl - 1)
    def _():
        signal(bar, {"fsdp": f + 2})

    @pl.when(p > 0)
    def _():
        signal(bar, {"fsdp": f - 2})

    pl.semaphore_wait(bar, 3 + jnp.where(p < nl - 1, 1, 0) + jnp.where(p > 0, 1, 0))

    rows = ins[4].shape[0] // SEQ
    half = D // 2
    cols = (slice(0, half), slice(half, D))
    first, second = (px, py), (py, px)

    def chunk(ref, i, a):
        return ref.at[pl.ds(i * rows, rows), cols[a]]

    def seq_one(t, a, m):
        i = (first[a] ^ second[a] ^ s) if m == 0 else first[a]
        return rcopy(
            chunk(ins[4 + t], i, a), ab[t].at[a, m], xs.at[t, a, m], xr.at[t, a, m], {"seq": first[a]}
        )

    def seq_two(t, a):
        return rcopy(az[t].at[a, 0], az[t].at[a, 1], xs.at[t, a, 2], xr.at[t, a, 2], {"seq": second[a]})

    shard = [ins[g].shape[0] // nf for g in range(4)]

    def piece(g, i):
        return ins[g].at[pl.ds(i * shard[g], shard[g])]

    def swap(g, q):
        return rcopy(piece(g, q * 2 + 1 - c), pb[g].at[q], zs.at[g, 0, q], zr.at[g, 0, q], {"fsdp": partner})

    def up(g, q):
        return rcopy(cs[g].at[q], ub[g].at[q], zs.at[g, 1, q], zr.at[g, 1, q], {"fsdp": f + 2})

    def down(g, q):
        return rcopy(cs[g].at[q], db[g].at[q], zs.at[g, 2, q], zr.at[g, 2, q], {"fsdp": f - 2})

    order = []
    for k in range(nl // 2):
        order += [nl - 1 - k, k]
    for g in range(4):
        for q in order:
            swap(g, q).start()
    for t in range(2):
        for m in range(2):
            for a in range(2):
                seq_one(t, a, m).start()

    def add(*terms):
        total = terms[0].astype(F32)
        for term in terms[1:]:
            total = total + term.astype(F32)
        return total

    def line(g):
        for q in order:
            swap(g, q).wait_recv()
            mine = piece(g, q * 2 + c)

            @pl.when(q > p)
            def _():
                @pl.when(p > 0)
                def _():
                    up(g, q).wait_recv()
                    cs[g][q] = add(mine[...], pb[g][q], ub[g][q]).astype(cs[g].dtype)

                @pl.when(p == 0)
                def _():
                    cs[g][q] = add(mine[...], pb[g][q]).astype(cs[g].dtype)

                up(g, q).start()

            @pl.when(q < p)
            def _():
                @pl.when(p < nl - 1)
                def _():
                    down(g, q).wait_recv()
                    cs[g][q] = add(mine[...], pb[g][q], db[g][q]).astype(cs[g].dtype)

                @pl.when(p == nl - 1)
                def _():
                    cs[g][q] = add(mine[...], pb[g][q]).astype(cs[g].dtype)

                down(g, q).start()

    def close(g):
        mine = piece(g, f)

        @pl.when(p > 0)
        def _():
            up(g, p).wait_recv()

        @pl.when(p < nl - 1)
        def _():
            down(g, p).wait_recv()

        @pl.when(p == 0)
        def _():
            own[g][...] = add(mine[...], pb[g][p], db[g][p]).astype(own[g].dtype)

        @pl.when(p == nl - 1)
        def _():
            own[g][...] = add(mine[...], pb[g][p], ub[g][p]).astype(own[g].dtype)

        @pl.when(jnp.logical_and(p > 0, p < nl - 1))
        def _():
            own[g][...] = add(mine[...], pb[g][p], ub[g][p], db[g][p]).astype(own[g].dtype)

    for g in range(4):
        line(g)
        if g == 1:
            for t in range(2):
                for a in range(2):
                    seq_one(t, a, 0).wait_recv()
                    az[t][a, 0] = add(chunk(ins[4 + t], second[a], a)[...], ab[t][a, 0]).astype(BF16)
                    seq_two(t, a).start()

    for g in range(4):
        close(g)
        n = shard[g]
        place = outs[g].at[pl.ds(s * n, n)]
        rcopy(own[g], place, as_.at[g, 0], ar.at[g, 0], {"seq": px}).start()
        rcopy(own[g], place, as_.at[g, 1], ar.at[g, 1], {"seq": py}).start()
        pltpu.make_async_copy(own[g], place, ls.at[g]).start()

    for t in range(2):
        for a in range(2):
            seq_one(t, a, 1).wait_recv()
            seq_two(t, a).wait_recv()
            outs[4 + t][:, cols[a]] = add(chunk(ins[4 + t], s, a)[...], ab[t][a, 1], az[t][a, 1])

    for g in range(4):
        seq_gather_relay(g, own[g], outs[g], as_, ar, px, py, s)
    for g in range(4):
        seq_gather_finish(g, own[g], outs[g], as_, ar, px, py, s)
        place = outs[g].at[pl.ds(s * shard[g], shard[g])]
        pltpu.make_async_copy(own[g], place, ls.at[g]).wait()
        for q in range(nl):
            swap(g, q).wait_send()

            @pl.when(q > p)
            def _():
                up(g, q).wait_send()

            @pl.when(q < p)
            def _():
                down(g, q).wait_send()

    for t in range(2):
        for a in range(2):
            seq_one(t, a, 0).wait_send()
            seq_one(t, a, 1).wait_send()
            seq_two(t, a).wait_send()


def reduce_all(nf, gv, gg, go, small, out_part, dn_part):
    shape = jax.ShapeDtypeStruct
    dma = pltpu.SemaphoreType.DMA
    nl = nf // 2
    groups = (small, gv, gg, go)
    rows = out_part.shape[0] // SEQ
    boxes = [((g.shape[0] // nf, g.shape[1]), g.dtype) for g in groups]
    lines = [pltpu.VMEM((nl,) + box, dtype) for box, dtype in boxes]
    return pl.pallas_call(
        functools.partial(reduce_kernel, nf),
        out_shape=[shape((SEQ * box[0], box[1]), dtype) for box, dtype in boxes] + [shape((rows, D), F32)] * 2,
        in_specs=[VMEM] * 6,
        out_specs=[VMEM] * 6,
        scratch_shapes=lines * 4
        + [pltpu.VMEM(box, dtype) for box, dtype in boxes]
        + [pltpu.VMEM((2, 2, rows, D // 2), BF16)] * 4
        + [
            dma((4, 3, nl)),
            dma((4, 3, nl)),
            dma((2, 2, 3)),
            dma((2, 2, 3)),
            dma((4, 4)),
            dma((4, 4)),
            dma((4,)),
        ],
        name="reduce_all",
        compiler_params=pltpu.CompilerParams(
            collective_id=3, has_side_effects=True, vmem_limit_bytes=VMEM_LIMIT
        ),
    )(small, gv, gg, go, out_part, dn_part)


def own_rows(array, index, row_count):
    return lax.dynamic_slice_in_dim(array, index * row_count, row_count, 0)


def pack(parts, nf):
    flat = jnp.concatenate([part.reshape(nf, -1) for part in parts], axis=1)
    rows = -(-flat.shape[1] // 1024) * 8
    flat = jnp.pad(flat, ((0, 0), (0, rows * 128 - flat.shape[1])))
    return flat.reshape(nf * rows, 128)


def unpack(packed, shapes, count):
    flat = packed.reshape(count, -1)
    out, at = [], 0
    for shape in shapes:
        size = 1
        for extent in shape:
            size *= extent
        size //= count
        out.append(flat[:, at : at + size].reshape(shape))
        at += size
    return out


def body(
    tokens,
    input_projection_weight,
    pre_gain,
    conv_weight,
    conv_bias,
    step_bias,
    decay_log,
    skip_gain,
    post_gain,
    output_projection_weight,
    cotangent,
):
    nf = lax.axis_size("fsdp")
    s = lax.axis_index("seq")
    tok = tokens.reshape(tokens.shape[1:])
    cot = cotangent.reshape(cotangent.shape[1:])
    win = input_projection_weight
    n = win.shape[0]

    w_gate = lax.dynamic_slice(win, (0, s * W), (n, W))
    w_mix = jnp.concatenate(
        [
            lax.dynamic_slice(win, (0, INNER + s * W), (n, W)),
            win[:, 2 * INNER : 2 * INNER + 2 * STATE],
            lax.dynamic_slice(win, (0, 2 * INNER + 2 * STATE + s * HL), (n, HL)),
            jnp.zeros((n, 128 - HL), BF16),
        ],
        axis=1,
    )
    w_out = own_rows(output_projection_weight, s, W).T
    small = pack(
        [
            v.astype(F32)
            for v in (pre_gain, conv_weight, conv_bias, step_bias, decay_log, skip_gain, post_gain)
        ],
        1,
    )
    tok_all, cot_all, w_mix, w_gate, w_out, small = gather_all(nf, tok, cot, w_mix, w_gate, w_out, small)
    shapes = ((D,), (XBC, 4), (XBC,), (HEADS,), (HEADS,), (HEADS,), (INNER,))
    pre, conv_w, conv_b, step_b, decay, skip, post = unpack(small, shapes, nf)
    kw = jnp.concatenate([conv_w.T, conv_b[None], jnp.zeros((3, XBC), F32)], axis=0)
    kw = jnp.concatenate([lax.dynamic_slice(kw, (0, s * W), (8, W)), kw[:, INNER:]], axis=1)
    per_head = jnp.stack([step_b, -jnp.exp(decay), skip])
    per_head = lax.dynamic_slice(per_head, (0, s * HL), (3, HL))
    hp = jnp.pad(per_head, ((0, 5), (0, 128 - HL)))
    ex = jnp.broadcast_to(jnp.repeat(per_head[2], HW)[None], (8, W))
    post = own_rows(post, s, W)

    residual = tok_all.astype(F32)
    rho0 = lax.rsqrt(jnp.mean(residual * residual, axis=-1, keepdims=True) + EPS)
    n0 = residual * rho0
    normed = (n0 * pre).astype(BF16)
    mix_raw = nn(normed, w_mix).astype(BF16)
    gate_raw = nn(normed, w_gate).astype(BF16)
    v_raw, s_raw, r_raw = mix_raw[:, :W], mix_raw[:, W:CH], mix_raw[:, CH:]
    mixed, k, st = scan_fwd(v_raw, s_raw, r_raw, kw, hp, ex)

    d_shaped = nn(cot_all, w_out)
    gate = gate_raw.astype(F32)
    mixed = mixed.astype(F32)
    sg = jax.nn.sigmoid(gate)
    sl = gate * sg
    gated = mixed * sl
    e1 = d_shaped * post
    sums = jnp.concatenate(
        [jnp.sum(gated * gated, axis=-1).reshape(-1, 128), jnp.sum(e1 * gated, axis=-1).reshape(-1, 128)]
    )
    sums = stats_sum(sums)
    half = sums.shape[0] // 2
    rho1 = lax.rsqrt(sums[:half].reshape(-1, 1) / INNER + EPS)
    mean1 = rho1 * sums[half:].reshape(-1, 1) / INNER
    n1 = gated * rho1
    shaped = (n1 * post).astype(BF16)
    g_post = jnp.sum(d_shaped * n1, axis=0)
    d_gated = rho1 * (e1 - n1 * mean1)
    d_mixed = (d_gated * sl).astype(BF16)
    d_gate = (d_gated * mixed * (sg * (1.0 + gate * (1.0 - sg)))).astype(BF16)

    out_part = nt(shaped, w_out).astype(BF16)
    tn = (((0,), (0,)), ((), ()))
    g_out = lax.dot_general(cot_all, shaped, tn, preferred_element_type=F32).astype(BF16)
    g_gate = lax.dot_general(normed, d_gate, tn, preferred_element_type=F32).astype(BF16)

    dv, g_conv, g_chan, g_head = scan_bwd(v_raw, s_raw, r_raw, k, d_mixed, st, kw, hp, ex)
    g_mix = lax.dot_general(normed, dv, tn, preferred_element_type=F32).astype(BF16)
    dn_part = nt(d_gate, w_gate) + nt(dv, w_mix)
    g_pre = jnp.sum(dn_part * n0, axis=0)

    def placed(full, piece, at):
        return lax.dynamic_update_slice_in_dim(jnp.zeros((full,) + piece.shape[1:], F32), piece, at, 0)

    g_cw = jnp.concatenate([placed(INNER, g_conv[:4, :W].T, s * W), g_conv[:4, W:].T])
    g_cb = jnp.concatenate([placed(INNER, g_conv[4, :W], s * W), g_conv[4, W:]])
    small = pack(
        [
            g_pre,
            g_cw,
            g_cb,
            placed(HEADS, g_head[0, :HL], s * HL),
            placed(HEADS, g_head[1, :HL], s * HL),
            placed(HEADS, jnp.sum(g_chan[0].reshape(HL, HW), axis=1), s * HL),
            placed(INNER, g_post, s * W),
        ],
        nf,
    )
    small, g_mix, g_gate, g_out, out_sum, dn = reduce_all(
        nf, g_mix, g_gate, g_out, small, out_part, dn_part.astype(BF16)
    )

    block_out = tok.astype(F32) + out_sum
    res = tok.astype(F32)
    r0 = lax.rsqrt(jnp.mean(res * res, axis=-1, keepdims=True) + EPS)
    m0 = res * r0
    e0 = dn * pre
    grad_tokens = cot.astype(F32) + r0 * (e0 - m0 * jnp.mean(e0 * m0, axis=-1, keepdims=True))

    g_mix = g_mix.reshape(SEQ, n, VC).astype(F32)
    g_gate = g_gate.reshape(SEQ, n, W).astype(F32)
    grad_in = jnp.concatenate(
        [g_gate[i] for i in range(SEQ)]
        + [g_mix[i, :, :W] for i in range(SEQ)]
        + [jnp.sum(g_mix[:, :, W:CH], axis=0)]
        + [g_mix[i, :, CH : CH + HL] for i in range(SEQ)],
        axis=1,
    )
    grad_out = jnp.swapaxes(g_out.reshape(SEQ, n, W), 1, 2).reshape(INNER, n).astype(F32)
    small = jnp.sum(small.reshape(SEQ, -1, 128), axis=0)
    shards = [(shape[0] // nf,) + shape[1:] for shape in shapes]
    grad_pre, grad_cw, grad_cb, grad_step, grad_decay, grad_skip, grad_post = unpack(small, shards, 1)
    return (
        block_out[None],
        grad_tokens[None],
        grad_in,
        grad_pre,
        grad_cw,
        grad_cb,
        grad_step,
        grad_decay,
        grad_skip,
        grad_post,
        grad_out,
    )


def solution(mesh):
    in_specs = (
        P("fsdp", "seq", None),
        P("fsdp", None),
        P("fsdp"),
        P("fsdp", None),
        P("fsdp"),
        P("fsdp"),
        P("fsdp"),
        P("fsdp"),
        P("fsdp"),
        P(None, "fsdp"),
        P("fsdp", "seq", None),
    )
    out_specs = (
        P("fsdp", "seq", None),
        P("fsdp", "seq", None),
        P("fsdp", None),
        P("fsdp"),
        P("fsdp", None),
        P("fsdp"),
        P("fsdp"),
        P("fsdp"),
        P("fsdp"),
        P("fsdp"),
        P(None, "fsdp"),
    )
    return jax.shard_map(body, mesh=mesh, in_specs=in_specs, out_specs=out_specs, check_vma=False)
```

time: 1470 us -> 383 us (0.26)
  waiting for transfers between devices: 782 us -> 0 us
  Pallas kernels: 0 us -> 262 us
  local copies, waits for them, and re-layouts: 188 us -> 41 us
  other arithmetic: 147 us -> 17.8 us
  matrix products: 182 us -> 53.5 us
  blocking collectives: 119 us -> 0 us
  starting transfers between devices: 25.6 us -> 0 us
  between operations: 21.1 us -> 1.25 us
    reduce_scatter x3 -> x0, waiting for transfers between devices: 475 us -> none  [the longest x1 388 us: body(): lax.psum_scatter(grad_in_full, 'fsdp', scatter_dimension=0, tiled=True)]
    pallas_call x0 -> x5, Pallas kernels: none -> 262 us  [the longest x1 124 us: reduce_all(): pl.pallas_call(functools.partial(reduce_kernel, nf), out_shape=[shape((SE...]
    dot_general x25 -> x9, matrix products: 182 us -> 53.5 us  [the longest x3 20.2 us: nn(): lax.dot_general(a, b, (((1,), (0,)), ((), ())), precision=precision, pref...]
    all_gather x2 -> x0, waiting for transfers between devices: 124 us -> none  [the longest x1 124 us: body(): lax.all_gather(input_projection_weight, 'fsdp', axis=0, tiled=True)]
    psum x1 -> x0, waiting for transfers between devices: 103 us -> none  [body(): lax.psum((shards[0], shards[1], shards[2], shards[3], shards[4], shards[5...]
    unnamed x7 -> x1, other arithmetic: 67.9 us -> 0.19 us
    unnamed x2 -> x0, blocking collectives: 56.4 us -> none
    all_to_all x6 -> x0, waiting for transfers between devices: 56.1 us -> none  [the longest x1 18.8 us: body(): lax.all_to_all(grad_mixed.astype(jnp.bfloat16), 'seq', split_axis=2, conc...]
  transfers between devices with their start and end apart: 13 -> 0, of which waited for: 9 -> 0; matrix products, arithmetic and copies ran while one was open for 20% -> 0% of each run, Pallas kernels for 0% -> 0%
where the time goes in v1:
time: 383 us; the launch traced here: 375 us
  Pallas kernels  262 us (68%)
  matrix products  53.5 us (14%)
  local copies, waits for them, and re-layouts  41 us (11%)
  other arithmetic  17.8 us (5%)
    pallas_call x1, Pallas kernels, reduce_all(): pl.pallas_call(functools.partial(reduce_kernel, nf), out_shape=[shape((SE...  124 us
    pallas_call x1, Pallas kernels, gather_all(): pl.pallas_call(functools.partial(gather_kernel, nf), out_shape=[shape((SE...  84.3 us
    pallas_call x1, Pallas kernels, scan_bwd(): pl.pallas_call(scan_bwd_kernel, out_shape=[shape((length, VC), BF16), sha...  30.7 us
    dot_general x3, matrix products, nn(): lax.dot_general(a, b, (((1,), (0,)), ((), ())), precision=precision, pref...  20.2 us
    pallas_call x1, Pallas kernels, scan_fwd(): pl.pallas_call(scan_fwd_kernel, out_shape=[shape((length, W), BF16), shap...  16.5 us
    dot_general x3, matrix products, nt(): lax.dot_general(a, b, (((1,), (1,)), ((), ())), precision=precision, pref...  13.5 us

profile of v1, /device:TPU:8, one launch (start us, length us, event | category | flops | bytes accessed | tf_op | source)
XLA Modules:
  0.0 375.3 jit_solution(14745156658203381339)
XLA Ops:
  1.5 1.4 fusion.20
  8.4 2.0 constant_dynamic-slice_fusion.2
  11.3 84.3 %gather_all.1 = (bf16[1024,1536]{1,0:T(8,128)(2,1)}, bf16[1024,1536]{1,0:T(8,128)(2,1)}, bf16[1536,1152]{1,0:T(8,128)(2,1)}, bf16[1536,768]{1,0:T(8,128)(2,1)}, ...) custom-call(bf16[256,1536]{1,0:T(8,128)(2,1)} %bitcast.85, bf16[256,1536]{1,0:T(8,128)(2,1)} %bitcast.86, ...), custom_call_target="tpu_custom_call" | custom-call | tf_op jit(solution)/shard_map/gather_all/pallas_call | solution.py:204
  96.5 2.6 fusion.4
  101.3 1.7 reshape.229
  104.3 7.4 %convolution_convert_fusion.2 = bf16[1024,1152]{1,0:T(8,128)(2,1)S(1)} fusion(bf16[1536,1152]{1,0:T(8,128)(2,1)} %get-tuple-element.32, bf16[1024,1536]{1,0:T(8,128)(2,1)} %get-tuple-element.30, f32[1536]{0:T(1024)S(1)} %mul.156, f32[1024]{0:T(1024)S(1)} %add_rsqrt_fusion), kind=kOutput, calls=%fused_computation.15 | convolution fusion | flops 3631349760 | bytes 9054208 | tf_op jit(solution)/shard_map/dot_general | solution.py:45
  114.5 4.3 %fusion.30 = f32[1024,768]{1,0:T(8,128)} fusion(bf16[1024,1536]{1,0:T(8,128)(2,1)S(1)} %copy-done.15, bf16[1536,768]{1,0:T(8,128)(2,1)S(1)} %copy-done.17), kind=kOutput, calls=%fused_computation.90 | convolution fusion | flops 2415919104 | bytes 8650752 | tf_op jit(solution)/shard_map/dot_general | solution.py:45
  118.8 16.5 %scan_fwd.1 = (bf16[1024,768]{1,0:T(8,128)(2,1)}, f32[1024,1024]{1,0:T(8,128)}, bf16[8,128,768]{2,1,0:T(8,128)(2,1)}) custom-call(bf16[1024,768]{1,0:T(8,128)(2,1)} %slice.173.v_ref, bf16[1024,256]{1,0:T(8,128)(2,1)} %slice.174.s_ref, bf16[1024,128]{1,0:T(8,128)(2,1)} %slice.175.r_ref, f32[8,1024]{1,0:T(8,128)} %pad_maximum_fusion.1.kw_ref, ...), custom_call_target="tpu_custom_call" | custom-call | tf_op jit(solution)/shard_map/scan_fwd/pallas_call | solution.py:329
  135.3 8.5 %multiply_reduce_fusion.2 = (f32[1024]{0:T(1024)S(1)}, f32[1024]{0:T(1024)S(1)}, bf16[1024,768]{1,0:T(8,128)(2,1)}) fusion(bf16[1024,768]{1,0:T(8,128)(2,1)} %get-tuple-element.33, f32[1024,768]{1,0:T(8,128)} %fusion.30, f32[768]{0:T(1024)S(1)} %dynamic_slice.27, bf16[1536,768]{1,0:T(8,128)(2,1)} %get-tuple-element.34, ...), kind=kOutput, calls=%fused_computation.30 | convolution fusion | flops 2432432128 | bytes 11817984 | tf_op jit(solution)/shard_map/dot_general | solution.py:45
  144.4 6.1 %stats_sum.1 = f32[16,128]{1,0:T(8,128)} custom-call(f32[16,128]{1,0:T(8,128)} %pad_maximum_fusion.3.a), custom_call_target="tpu_custom_call" | custom-call | tf_op jit(solution)/shard_map/stats_sum/pallas_call | solution.py:246
  151.2 7.0 %convolution_convert_fusion.3.refs_3_ = bf16[1536,768]{1,0:T(8,128)(2,1)} fusion(bf16[1024,1536]{1,0:T(8,128)(2,1)} %get-tuple-element.35, f32[1024]{0:T(1024)S(1)} %rsqrt_bitcast_fusion, f32[768]{0:T(1024)S(1)} %dynamic_slice.27, bf16[1024,768]{1,0:T(8,128)(2,1)S(1)} %copy-done.9, bf16[1024,768]{1,0:T(8,128)(2,1)} %get-tuple-element.100), kind=kOutput, calls=%fused_computation.16 | convolution fusion | flops 2424963072 | bytes 8657920 | tf_op jit(solution)/shard_map/dot_general | solution.py:794
  158.3 4.1 %multiply_convert_fusion.1 = (bf16[1024,768]{1,0:T(8,128)(2,1)}, bf16[1024,768]{1,0:T(8,128)(2,1)}, f32[768]{0:T(1024)S(1)}) fusion(f32[1024]{0:T(1024)S(1)} %fusion.22, f32[1024,768]{1,0:T(8,128)S(1)} %copy-done.6, f32[1024]{0:T(1024)S(1)} %rsqrt_bitcast_fusion, f32[768]{0:T(1024)S(1)} %dynamic_slice.27, bf16[1024,768]{1,0:T(8,128)(2,1)S(1)} %copy-done.10, ...), kind=kLoop, calls=%fused_computation.27 | loop fusion | flops 18087168 | bytes 9451520 | tf_op jit(solution)/shard_map/convert_element_type | solution.py:789
  162.3 4.9 %convolution_convert_fusion.1.refs_4_ = bf16[1024,1536]{1,0:T(8,128)(2,1)} fusion(bf16[1536,768]{1,0:T(8,128)(2,1)S(1)} %copy-done.18, f32[1024]{0:T(1024)S(1)} %rsqrt_bitcast_fusion, f32[768]{0:T(1024)S(1)} %dynamic_slice.27, bf16[1024,768]{1,0:T(8,128)(2,1)S(1)} %copy-done.9, bf16[1024,768]{1,0:T(8,128)(2,1)S(1)} %copy-done.10), kind=kOutput, calls=%fused_computation.14 | convolution fusion | flops 2425356288 | bytes 8657920 | tf_op jit(solution)/shard_map/dot_general | solution.py:49
  167.2 30.7 %scan_bwd.1 = (bf16[1024,1152]{1,0:T(8,128)(2,1)}, f32[8,1024]{1,0:T(8,128)}, f32[8,768]{1,0:T(8,128)}, f32[8,128]{1,0:T(8,128)}) custom-call(bf16[1024,768]{1,0:T(8,128)(2,1)} %slice.173.v_ref, bf16[1024,256]{1,0:T(8,128)(2,1)} %slice.174.s_ref, bf16[1024,128]{1,0:T(8,128)(2,1)} %slice.175.r_ref, f32[1024,1024]{1,0:T(8,128)} %get-tuple-element.37.k_ref, ...), custom_call_target="tpu_custom_call" | custom-call | tf_op jit(solution)/shard_map/scan_bwd/pallas_call | solution.py:464
  206.0 6.8 %convolution_convert_fusion.4.refs_2_ = bf16[1536,768]{1,0:T(8,128)(2,1)} fusion(bf16[1024,768]{1,0:T(8,128)(2,1)} %get-tuple-element.74, bf16[1024,1536]{1,0:T(8,128)(2,1)} %get-tuple-element.30, f32[1536]{0:T(1024)S(1)} %mul.156, f32[1024]{0:T(1024)S(1)} %add_rsqrt_fusion), kind=kOutput, calls=%fused_computation.17 | convolution fusion | flops 2423390208 | bytes 7088128 | tf_op jit(solution)/shard_map/dot_general | solution.py:795
  212.8 2.6 fusion.31
  216.4 6.0 %fusion.27 = (bf16[1024,1536]{1,0:T(8,128)(2,1)}, f32[1536]{0:T(1024)S(1)}) fusion(f32[1024]{0:T(1024)S(1)} %add_rsqrt_fusion, bf16[1024,1536]{1,0:T(8,128)(2,1)S(1)} %copy-done.5, f32[1024,1536]{1,0:T(8,128)S(1)} %fusion.31, bf16[1024,1152]{1,0:T(8,128)(2,1)S(1)} %copy-done.19, bf16[1536,1152]{1,0:T(8,128)(2,1)S(1)} %copy-done.14), kind=kOutput, calls=%fused_computation.87 | convolution fusion | flops 3633314304 | bytes 18491392 | tf_op jit(solution)/shard_map/dot_general | solution.py:49
  222.4 6.0 %convolution_convert_fusion.refs_1_ = bf16[1536,1152]{1,0:T(8,128)(2,1)} fusion(bf16[1024,1152]{1,0:T(8,128)(2,1)S(1)} %copy-done.19, bf16[1024,1536]{1,0:T(8,128)(2,1)S(1)} %copy-done.5, f32[1536]{0:T(1024)S(1)} %mul.156, f32[1024]{0:T(1024)S(1)} %add_rsqrt_fusion), kind=kOutput, calls=%fused_computation.2 | convolution fusion | flops 3631939584 | bytes 9054208 | tf_op jit(solution)/shard_map/dot_general | solution.py:798
  229.3 124.1 %reduce_all.1 = (f32[96,128]{1,0:T(8,128)}, bf16[768,1152]{1,0:T(8,128)(2,1)}, bf16[768,768]{1,0:T(8,128)(2,1)}, bf16[768,768]{1,0:T(8,128)(2,1)}, f32[256,1536]{1,0:T(8,128)}, /*index=5*/f32[256,1536]{1,0:T(8,128)}) custom-call(f32[192,128]{1,0:T(8,128)} %reshape.241.refs_0_, bf16[1536,1152]{1,0:T(8,128)(2,1)} %convolution_convert_fusion.refs_1_, ...), custom_call_target="tpu_custom_call" | custom-call | tf_op jit(solution)/shard_map/reduce_all/pallas_call | solution.py:665
  353.4 1.9 fusion.14
  355.3 4.0 %fusion.18 = (f32[1,256,1536]{2,1,0:T(8,128)}, f32[1,256,1536]{2,1,0:T(8,128)}) fusion(f32[256,1536]{1,0:T(8,128)S(1)} %copy-done.3, f32[256]{0:T(256)S(1)} %broadcast_multiply_fusion, f32[1536]{0:T(1024)S(1)} %mul.156, f32[256]{0:T(256)S(1)} %add_rsqrt_fusion.1, bf16[1,256,1536]{2,1,0:T(8,128)(2,1)} %param.21, bf16[1,256,1536]{2,1,0:T(8,128)(2,1)S(1)} %copy-done.2, ...), kind=kLoop, calls=%fused_computation.42 | loop fusion | flops 3538944 | bytes 7872512 | tf_op jit(solution)/shard_map/broadcast_in_dim | solution.py:845
  363.0 1.7 copy.40
  367.8 1.5 slice_bitcast_fusion
  369.3 5.8 %concatenate.36 = f32[192,6448]{1,0:T(8,128)} concatenate(f32[192,768]{1,0:T(8,128)S(1)} %get-tuple-element.91, f32[192,768]{1,0:T(8,128)S(1)} %get-tuple-element.90, f32[192,768]{1,0:T(8,128)S(1)} %get-tuple-element.89, f32[192,768]{1,0:T(8,128)S(1)} %get-tuple-element.88, f32[192,768]{1,0:T(8,128)} %get-tuple-element.85, f32[192,768]{1,0:T(8,128)} %get-tuple-element.84, ...), dimensions={1} | concatenate | bytes 9904128 | tf_op jit(solution)/shard_map/concatenate | solution.py:832
  (132 shorter events, 32.4 us)
Async XLA Ops:
  0.6 7.0 %copy-start = (bf16[3072,192]{0,1:T(8,128)(2,1)S(1)}, bf16[3072,192]{0,1:T(8,128)(2,1)}, u32[]{:S(2)}) copy-start(bf16[3072,192]{0,1:T(8,128)(2,1)} %param.20) | copy-start | bytes 3538948
  0.7 9.8 %slice-start = ((bf16[192,6448]{1,0:T(8,128)(2,1)}), bf16[192,256]{1,0:T(8,128)(2,1)S(1)}, s32[]{:S(2)}) async-start(bf16[192,6448]{1,0:T(8,128)(2,1)} %param.12), calls=%async_computation | async-start | bytes 196608 | tf_op jit(solution)/shard_map/slice | solution.py:737
  104.3 10.2 %copy-start.17 = (bf16[1536,768]{1,0:T(8,128)(2,1)S(1)}, bf16[1536,768]{1,0:T(8,128)(2,1)}, u32[]{:S(2)}) copy-start(bf16[1536,768]{1,0:T(8,128)(2,1)} %get-tuple-element.36) | copy-start | bytes 7077892
  111.7 2.8 copy-start.15
  135.3 15.9 %copy-start.9 = (bf16[1024,768]{1,0:T(8,128)(2,1)S(1)}, bf16[1024,768]{1,0:T(8,128)(2,1)}, u32[]{:S(2)}) copy-start(bf16[1024,768]{1,0:T(8,128)(2,1)} %get-tuple-element.33) | copy-start | bytes 4718596
  151.2 7.1 %copy-start.12 = (f32[16,128]{1,0:T(8,128)S(1)}, f32[16,128]{1,0:T(8,128)}, u32[]{:S(2)}) copy-start(f32[16,128]{1,0:T(8,128)} %stats_sum.1) | copy-start | bytes 24580
  151.2 7.1 %copy-start.6 = (f32[1024,768]{1,0:T(8,128)S(1)}, f32[1024,768]{1,0:T(8,128)}, u32[]{:S(2)}) copy-start(f32[1024,768]{1,0:T(8,128)} %fusion.30) | copy-start | bytes 9437188
  151.2 7.1 %copy-start.10 = (bf16[1024,768]{1,0:T(8,128)(2,1)S(1)}, bf16[1024,768]{1,0:T(8,128)(2,1)}, u32[]{:S(2)}) copy-start(bf16[1024,768]{1,0:T(8,128)(2,1)} %get-tuple-element.100) | copy-start | bytes 4718596
  158.2 4.1 %copy-start.18 = (bf16[1536,768]{1,0:T(8,128)(2,1)S(1)}, bf16[1536,768]{1,0:T(8,128)(2,1)}, u32[]{:S(2)}) copy-start(bf16[1536,768]{1,0:T(8,128)(2,1)} %get-tuple-element.36) | copy-start | bytes 7077892
  206.0 6.8 %copy-start.8 = (bf16[1024,768]{1,0:T(8,128)(2,1)S(1)}, bf16[1024,768]{1,0:T(8,128)(2,1)}, u32[]{:S(2)}) copy-start(bf16[1024,768]{1,0:T(8,128)(2,1)} %get-tuple-element.74) | copy-start | bytes 4718596
  206.0 6.8 %copy-start.16 = (bf16[1536,768]{1,0:T(8,128)(2,1)S(1)}, bf16[1536,768]{1,0:T(8,128)(2,1)}, u32[]{:S(2)}) copy-start(bf16[1536,768]{1,0:T(8,128)(2,1)} %get-tuple-element.34) | copy-start | bytes 7077892
  212.8 2.7 copy-start.5
  212.8 3.0 copy-start.14
  212.8 3.6 copy-start.19
  229.3 124.1 %copy-start.2 = (bf16[1,256,1536]{2,1,0:T(8,128)(2,1)S(1)}, bf16[1,256,1536]{2,1,0:T(8,128)(2,1)}, u32[]{:S(2)}) copy-start(bf16[1,256,1536]{2,1,0:T(8,128)(2,1)} %param.11) | copy-start | bytes 2359300
  353.4 1.9 copy-start.3
  355.3 4.0 %copy-start.13 = (f32[96,128]{1,0:T(8,128)S(1)}, f32[96,128]{1,0:T(8,128)}, u32[]{:S(2)}) copy-start(f32[96,128]{1,0:T(8,128)} %get-tuple-element.47) | copy-start | bytes 147460
  355.3 7.5 %copy-start.11 = (bf16[768,768]{1,0:T(8,128)(2,1)S(1)}, bf16[768,768]{1,0:T(8,128)(2,1)}, u32[]{:S(2)}) copy-start(bf16[768,768]{1,0:T(8,128)(2,1)} %get-tuple-element.48) | copy-start | bytes 3538948
  363.0 1.7 copy-start.4
  364.7 1.5 copy-start.7
  369.3 5.8 %copy-start.1 = (bf16[3072,192]{0,1:T(8,128)(2,1)S(1)}, bf16[3072,192]{0,1:T(8,128)(2,1)}, u32[]{:S(2)}) copy-start(bf16[3072,192]{0,1:T(8,128)(2,1)} %param.20) | copy-start | bytes 3538948
